TPU v7x, 32 devices: a whole 2x2x4 slice. The times are simulated.
32 devices in a mesh: groups: 2 (over y), dp: 4 (over z), section: 2 (over x), tensor: 2 (over core).
Axes of the slice: x: 2, y: 2, z: 4, core: 2. Of those that a mesh axis runs over, the one named last changes fastest.
Arguments:
- hidden: bfloat16 [128, 8, 5120], P(('groups', 'dp')), parts along dimension 0, may hold values from -6 to 6
- unembed: bfloat16 [128, 8, 5120], P(('groups', 'dp')), parts along dimension 0, may hold values from -0.02734375 to 0.02734375
- value_proj: bfloat16 [2, 5120, 512], P('section', 'dp', 'tensor'), may hold values from -0.078125 to 0.078125
- output_proj: bfloat16 [2, 512, 5120], P('section', 'tensor', 'dp'), may hold values from -0.125 to 0.125
- norm_gains: float32 [2, 5120], P('section'), may hold values from 0.1 to 1.9
- survive: int32 [8], P(('groups', 'dp')), parts along dimension 0, may hold values from 0 to 1, as said below
- lengths: int32 [128], P(('groups', 'dp')), parts along dimension 0, may hold values from 1 to 8
- assign: int32 [128], P(('groups', 'dp')), parts along dimension 0, may hold values from 0 to 16, as said below
- advantage: float32 [128], P(('groups', 'dp')), parts along dimension 0, may hold values from -4 to 4
- reference_logit: float32 [128, 8], P(('groups', 'dp')), parts along dimension 0, may hold values from -4 to 4
- recorded_gap: float32 [128, 8], P(('groups', 'dp')), parts along dimension 0, may hold values from -2 to 2
Outputs:
- grad_value: float32 [4, 5120, 512], P(('groups', 'section'), 'dp', 'tensor'), parts along dimension 0
- grad_output: float32 [4, 512, 5120], P(('groups', 'section'), 'tensor', 'dp'), parts along dimension 0
There are 2 independent parts, one for each index of `groups`. A program takes and returns all parts, laid end to end along the dimension named above; an argument that names none is the same for every part. Nothing has to cross between parts.
Inputs may be any that keep to these rules, and one draw needn't show every extreme that they name: `survive`: 1 where the group of 16 responses is kept, 0 where it is dropped; in every draw all groups of some dp index are kept. `assign`: the 16 slots of a dp index list the local positions (0 to 15) of the responses of its kept groups, each exactly once, then hold 16 in every other slot.
All inputs are finite; a program needn't handle non-finite values.
Results may differ from a plain program's by a relative error of at most 0.029.
Values may be sent and summed in bfloat16 or wider, within the bound.
A program may use at most 64 MiB of HBM per device.

v0:
```python
import math
import jax
import jax.numpy as jnp
from jax import lax
from jax.sharding import PartitionSpec as P

GROUP = 16
MB_RESP = 8
eps_norm = 1e-06
loss_scale = 4096.0
clip_high = math.log(1.28)
clip_low = math.log(0.8)


def from_behind(block, axis, distance):
    devices = range(lax.axis_size(axis))
    route = [(i - distance, i) for i in devices if i - distance in devices]
    return lax.ppermute(block, axis, route)


def norm_forward(row_block, norm_gain):
    values = row_block.astype(jnp.float32)
    inverse = lax.rsqrt(jnp.mean(values * values, axis=-1, keepdims=True) + eps_norm)
    return (values, inverse, (values * inverse * norm_gain).astype(jnp.bfloat16))


def norm_backward(values, inverse, norm_gain, upstream):
    scaled = upstream * norm_gain
    inner_sum = jnp.sum(scaled * values, axis=-1, keepdims=True) / values.shape[-1]
    return inverse * scaled - values * (inverse * inverse * inverse) * inner_sum


def contract_last(left_rows, right_rows):
    return lax.dot_general(
        left_rows, right_rows, (((1,), (1,)), ((), ())), preferred_element_type=jnp.float32
    )


def contract_first(left_rows, right_rows):
    return lax.dot_general(
        left_rows, right_rows, (((0,), (0,)), ((), ())), preferred_element_type=jnp.float32
    )


def take_slot(slot_store, slot_index):
    return lax.dynamic_index_in_dim(slot_store, slot_index, 0, keepdims=False)


def put_slot(slot_store, new_value, slot_index, active):
    previous = take_slot(slot_store, slot_index)
    return lax.dynamic_update_index_in_dim(
        slot_store, jnp.where(active, new_value, previous), slot_index, 0
    )


def local(
    hidden,
    unembed,
    value_proj,
    output_proj,
    norm_gains,
    survive,
    lengths,
    assign,
    advantage,
    reference_logit,
    recorded_gap,
):
    resp_count = hidden.shape[0]
    positions = hidden.shape[1]
    model_width = hidden.shape[2]
    half_value = value_proj.shape[2]
    micro_count = resp_count // MB_RESP
    row_count = MB_RESP * positions
    section_count = lax.axis_size("section")
    section_index = lax.axis_index("section")
    is_last = section_index == section_count - 1
    norm_gain = norm_gains[0]
    alive_mask = jnp.repeat(survive, GROUP)
    local_count = jnp.sum((alive_mask * lengths).astype(jnp.float32))
    gathered_value, gathered_output = (
        lax.all_gather(value_proj, "dp", axis=1, tiled=True),
        lax.all_gather(output_proj, "dp", axis=2, tiled=True),
    )
    w_first = gathered_value[0]
    w_second = gathered_output[0]

    def pick(array):
        return jnp.take(array, assign, axis=0, mode="fill", fill_value=0)

    slot_hidden = pick(hidden).reshape(micro_count, row_count, model_width)
    slot_unembed = pick(unembed).reshape(micro_count, row_count, model_width)
    position_index = lax.broadcasted_iota(jnp.int32, (resp_count, positions), 1)
    live_mask = (position_index < pick(lengths)[:, None]).astype(jnp.float32)
    advantages = jnp.broadcast_to(pick(advantage)[:, None], (resp_count, positions))
    gap_rows = pick(recorded_gap)
    clipped = (advantages > 0) & (gap_rows > clip_high) | (advantages < 0) & (gap_rows < clip_low)
    kept_mask = 1.0 - clipped.astype(jnp.float32)
    weight_rows = (-loss_scale * advantages * kept_mask * live_mask).reshape(micro_count, row_count)
    logit_base = pick(reference_logit).reshape(micro_count, row_count)
    step_count = micro_count + section_count - 1
    store_in = jnp.zeros((micro_count, row_count, model_width), jnp.bfloat16)
    store_normed = jnp.zeros((micro_count, row_count, model_width), jnp.bfloat16)
    store_projected = jnp.zeros((micro_count, row_count, half_value), jnp.bfloat16)
    store_out = jnp.zeros((micro_count, row_count, model_width), jnp.bfloat16)
    arriving = jnp.zeros((row_count, model_width), jnp.bfloat16)
    for step_index in range(step_count):
        micro_index = step_index - section_index
        active = (micro_index >= 0) & (micro_index < micro_count)
        clamped = jnp.clip(micro_index, 0, micro_count - 1)
        entering = jnp.where(section_index == 0, take_slot(slot_hidden, clamped), arriving)
        values, inverse, normed = norm_forward(entering, norm_gain)
        projected = jnp.dot(normed, w_first, preferred_element_type=jnp.float32).astype(
            jnp.bfloat16
        )
        partial_out = jnp.dot(projected, w_second, preferred_element_type=jnp.float32)
        mixed_sum = lax.psum(partial_out.astype(jnp.bfloat16), "tensor").astype(jnp.float32)
        leaving = (values + mixed_sum).astype(jnp.bfloat16)
        store_in = put_slot(store_in, entering, clamped, active)
        store_normed = put_slot(store_normed, normed, clamped, active)
        store_projected = put_slot(store_projected, projected, clamped, active)
        store_out = put_slot(store_out, leaving, clamped, active)
        arriving = from_behind(leaving, "section", 1)
    store_upstream = jnp.zeros((micro_count, row_count, model_width), jnp.bfloat16)
    store_grad_value = jnp.zeros((micro_count, row_count, half_value), jnp.bfloat16)
    arriving = jnp.zeros((row_count, model_width), jnp.bfloat16)
    for step_index in range(step_count):
        micro_index = step_index - (section_count - 1 - section_index)
        active = (micro_index >= 0) & (micro_index < micro_count)
        clamped = jnp.clip(micro_index, 0, micro_count - 1)
        top_rows = take_slot(store_out, clamped).astype(jnp.float32)
        unembed_rows = take_slot(slot_unembed, clamped).astype(jnp.float32)
        logit = jnp.sum(top_rows * unembed_rows, axis=-1)
        seed_rows = take_slot(weight_rows, clamped) * jnp.exp(
            logit - take_slot(logit_base, clamped)
        )
        start_grad = (seed_rows[:, None] * unembed_rows).astype(jnp.bfloat16)
        upstream = jnp.where(is_last, start_grad, arriving)
        entering = take_slot(store_in, clamped)
        normed = take_slot(store_normed, clamped)
        projected = take_slot(store_projected, clamped)
        grad_projected = contract_last(upstream, w_second).astype(jnp.bfloat16)
        partial_norm = contract_last(grad_projected, w_first)
        grad_normed = lax.psum(partial_norm.astype(jnp.bfloat16), "tensor").astype(jnp.float32)
        values, inverse, unused_normed = norm_forward(entering, norm_gain)
        grad_entering = (
            upstream.astype(jnp.float32) + norm_backward(values, inverse, norm_gain, grad_normed)
        ).astype(jnp.bfloat16)
        store_upstream = put_slot(store_upstream, upstream, clamped, active)
        store_grad_value = put_slot(store_grad_value, grad_projected, clamped, active)
        arriving = from_behind(grad_entering, "section", -1)
    flat_normed = store_normed.reshape(micro_count * row_count, model_width)
    flat_upstream = store_upstream.reshape(micro_count * row_count, model_width)
    flat_grad_value = store_grad_value.reshape(micro_count * row_count, half_value)
    flat_projected = store_projected.reshape(micro_count * row_count, half_value)
    reduced = lax.psum_scatter(
        jnp.concatenate(
            [
                contract_first(flat_normed, flat_grad_value),
                contract_first(flat_upstream, flat_projected),
            ],
            axis=1,
        ).astype(jnp.bfloat16),
        "dp",
        scatter_dimension=0,
        tiled=True,
    ).astype(jnp.float32)
    token_total = lax.psum(local_count, "dp")
    scaled_grads = reduced / token_total
    grad_value = scaled_grads[:, :half_value][None]
    grad_output = scaled_grads[:, half_value:].T[None]
    return (grad_value, grad_output)


def solution(mesh):
    placed = (
        P(("groups", "dp"), None, None),
        P(("groups", "dp"), None, None),
        P("section", "dp", "tensor"),
        P("section", "tensor", "dp"),
        P("section", None),
        P(("groups", "dp")),
        P(("groups", "dp")),
        P(("groups", "dp")),
        P(("groups", "dp")),
        P(("groups", "dp"), None),
        P(("groups", "dp"), None),
    )
    return jax.shard_map(
        local,
        mesh=mesh,
        in_specs=placed,
        out_specs=(
            P(("groups", "section"), "dp", "tensor"),
            P(("groups", "section"), "tensor", "dp"),
        ),
        check_vma=False,
    )
```

profile of v0, /device:TPU:0, one launch (start us, length us, event | category | flops | bytes accessed | tf_op | source)
XLA Modules:
  0.0 449.3 jit_solution(629598408572374933)
XLA Ops:
  9.5 1.7 gather_fusion.2
  14.8 2.0 broadcast_select_fusion.1
  18.2 48.9 %all-gather.3.cloned.1.call-done = bf16[1,5120,256]{2,1,0:T(8,128)(2,1)} async-done(((bf16[1,1280,256]{2,1,0:T(8,128)(2,1)}), bf16[1,5120,256]{2,1,0:T(8,128)(2,1)}) %all-gather.3.cloned.1.call-update) | async-done | bytes 2621456 | tf_op jit(solution)/shard_map/all_gather | solution.py:82
  67.1 2.6 bitcast_dynamic-update-slice_fusion.10
  69.7 52.5 %all-gather.5.cloned.1.call-done = bf16[1,256,5120]{2,1,0:T(8,128)(2,1)} async-done(((bf16[1,256,1280]{2,1,0:T(8,128)(2,1)}), bf16[1,256,5120]{2,1,0:T(8,128)(2,1)}) %all-gather.5.cloned.1.call-update) | async-done | bytes 2621456 | tf_op jit(solution)/shard_map/all_gather | solution.py:83
  122.2 3.2 convolution_convert_fusion.4
  128.5 14.6 %all-reduce.6.cloned.1.call-done = bf16[64,5120]{1,0:T(8,128)(2,1)} async-done(((bf16[64,5120]{1,0:T(8,128)(2,1)}), bf16[64,5120]{1,0:T(8,128)(2,1)}) %all-reduce.6.cloned.1.call-update) | async-done | bytes 655376 | tf_op jit(solution)/shard_map/psum | solution.py:117
  145.8 3.7 collective-permute-start
  150.7 13.2 %collective-permute-done = bf16[64,5120]{1,0:T(8,128)(2,1)S(1)} collective-permute-done((bf16[64,5120]{1,0:T(8,128)(2,1)S(1)}, bf16[64,5120]{1,0:T(8,128)(2,1)S(1)}, u32[]{:S(2)}, u32[]{:S(2)}) %collective-permute-start) | collective-permute-done | bytes 655392 | tf_op jit(solution)/shard_map/ppermute | solution.py:18
  168.6 2.0 constant_dynamic-slice_fusion.14
  170.6 2.0 constant_dynamic-slice_fusion.8
  172.6 16.8 %all-reduce.8.cloned.1.call-done = bf16[64,5120]{1,0:T(8,128)(2,1)} async-done(((bf16[64,5120]{1,0:T(8,128)(2,1)}), bf16[64,5120]{1,0:T(8,128)(2,1)}) %all-reduce.8.cloned.1.call-update) | async-done | bytes 655376 | tf_op jit(solution)/shard_map/psum | solution.py:117
  189.4 2.5 bitcast_dynamic-update-slice_fusion.4
  191.9 3.7 collective-permute-start.1
  195.6 2.2 constant_dynamic-slice_fusion.13
  197.8 12.1 %collective-permute-done.1 = bf16[64,5120]{1,0:T(8,128)(2,1)S(1)} collective-permute-done((bf16[64,5120]{1,0:T(8,128)(2,1)S(1)}, bf16[64,5120]{1,0:T(8,128)(2,1)S(1)}, u32[]{:S(2)}, u32[]{:S(2)}) %collective-permute-start.1) | collective-permute-done | bytes 655392 | tf_op jit(solution)/shard_map/ppermute | solution.py:18
  219.3 17.0 %all-reduce.10.cloned.1.call-done = bf16[64,5120]{1,0:T(8,128)(2,1)} async-done(((bf16[64,5120]{1,0:T(8,128)(2,1)}), bf16[64,5120]{1,0:T(8,128)(2,1)}) %all-reduce.10.cloned.1.call-update) | async-done | bytes 655376 | tf_op jit(solution)/shard_map/psum | solution.py:117
  236.2 3.1 bitcast_dynamic-update-slice_fusion.6
  239.3 2.4 fusion.32
  243.5 1.7 convolution_convert_fusion.1
  247.6 17.8 %all-reduce.12.cloned.1.call-done = bf16[64,5120]{1,0:T(8,128)(2,1)} async-done(((bf16[64,5120]{1,0:T(8,128)(2,1)}), bf16[64,5120]{1,0:T(8,128)(2,1)}) %all-reduce.12.cloned.1.call-update) | async-done | bytes 655376 | tf_op jit(solution)/shard_map/psum | solution.py:144
  265.4 2.1 fusion.48
  271.8 16.1 %collective-permute-done.2 = bf16[64,5120]{1,0:T(8,128)(2,1)S(1)} collective-permute-done((bf16[64,5120]{1,0:T(8,128)(2,1)S(1)}, bf16[64,5120]{1,0:T(8,128)(2,1)S(1)}, u32[]{:S(2)}, u32[]{:S(2)}) %collective-permute-start.2) | collective-permute-done | bytes 655392 | tf_op jit(solution)/shard_map/ppermute | solution.py:18
  291.7 1.7 convolution_convert_fusion
  293.5 19.2 %all-reduce.14.cloned.1.call-done = bf16[64,5120]{1,0:T(8,128)(2,1)} async-done(((bf16[64,5120]{1,0:T(8,128)(2,1)}), bf16[64,5120]{1,0:T(8,128)(2,1)}) %all-reduce.14.cloned.1.call-update) | async-done | bytes 655376 | tf_op jit(solution)/shard_map/psum | solution.py:144
  314.4 1.7 fusion.52
  318.6 16.3 %collective-permute-done.3 = bf16[64,5120]{1,0:T(8,128)(2,1)S(1)} collective-permute-done((bf16[64,5120]{1,0:T(8,128)(2,1)S(1)}, bf16[64,5120]{1,0:T(8,128)(2,1)S(1)}, u32[]{:S(2)}, u32[]{:S(2)}) %collective-permute-start.3) | collective-permute-done | bytes 655392 | tf_op jit(solution)/shard_map/ppermute | solution.py:18
  338.3 2.2 fusion.1
  340.5 2.7 pad_maximum_fusion
  344.5 12.9 %psum.47 = f32[]{:T(128)} all-reduce(f32[]{:T(128)} %convert_reduce_fusion), channel_id=1, replica_groups=mesh['groups'=2,'dp'=4,'section'=2,'tensor'=2] {'dp'}, use_global_device_ids=true, to_apply=%region_17.20 | all-reduce | flops 1 | bytes 8 | tf_op jit(solution)/shard_map/psum | solution.py:168
  357.4 80.2 %reduce-scatter.2.cloned.1.call-done = bf16[1280,512]{0,1:T(8,128)(2,1)} async-done(((bf16[5120,512]{0,1:T(8,128)(2,1)}), bf16[1280,512]{0,1:T(8,128)(2,1)}) %reduce-scatter.2.cloned.1.call-update) | async-done | bytes 1310736 | tf_op jit(solution)/shard_map/reduce_scatter | solution.py:156
  437.6 2.2 convert_divide_fusion
  (142 shorter events, 51.0 us)
Async XLA Ops:
  7.2 2.3 copy-start
  7.2 59.9 %all-gather.3.cloned.1.call-start = ((), (), s32[]{:S(2)}) async-start(), calls=%async_computation.1 | async-start | bytes 3276800 | tf_op jit(solution)/shard_map/all_gather | solution.py:82
  7.9 114.3 %all-gather.5.cloned.1.call-start = ((), (), s32[]{:S(2)}) async-start(), calls=%async_computation.2 | async-start | bytes 3276800 | tf_op jit(solution)/shard_map/all_gather | solution.py:83
  8.7 134.4 %all-reduce.6.cloned.1.call-start = ((), (), s32[]{:S(2)}) async-start(), calls=%async_computation.3 | async-start | bytes 1310720 | tf_op jit(solution)/shard_map/psum | solution.py:117
  9.5 1.7 copy-start.27
  11.2 2.4 copy-start.28
  11.2 3.0 copy-start.29
  14.8 52.3 %copy-start.26 = (f32[1,5120]{1,0:T(1,128)S(1)}, f32[1,5120]{1,0:T(1,128)}, u32[]{:S(2)}) copy-start(f32[1,5120]{1,0:T(1,128)} %param.19) | copy-start | bytes 61444
  125.4 64.0 %all-reduce.8.cloned.1.call-start = ((), (), s32[]{:S(2)}) async-start(), calls=%async_computation.4 | async-start | bytes 1310720 | tf_op jit(solution)/shard_map/psum | solution.py:117
  125.7 1.8 copy-start.13
  145.8 4.9 %copy-start.20 = (bf16[2,64,5120]{2,1,0:T(8,128)(2,1)}, bf16[2,64,5120]{2,1,0:T(8,128)(2,1)S(1)}, u32[]{:S(2)}) copy-start(bf16[2,64,5120]{2,1,0:T(8,128)(2,1)S(1)} %get-tuple-element.22) | copy-start | bytes 3932164
  145.8 18.1 %collective-permute-start = (bf16[64,5120]{1,0:T(8,128)(2,1)S(1)}, bf16[64,5120]{1,0:T(8,128)(2,1)S(1)}, u32[]{:S(2)}, u32[]{:S(2)}) collective-permute-start(bf16[64,5120]{1,0:T(8,128)(2,1)S(1)} %get-tuple-element.23), channel_id=1, source_target_pairs={{0,2},{1,3},{4,6},{5,7},{8,10},{9,11},{12,14},{13,15},{16,18},{17,... | collective-permute-start | bytes 1966088 | tf_op jit(solution)/shard_map/ppermute | solution.py:18
  150.7 14.6 %copy-start.8 = (bf16[1,5120,256]{2,1,0:T(8,128)(2,1)S(1)}, bf16[1,5120,256]{2,1,0:T(8,128)(2,1)}, u32[]{:S(2)}) copy-start(bf16[1,5120,256]{2,1,0:T(8,128)(2,1)} %all-gather.3.cloned.1.call-done) | copy-start | bytes 7864324
  165.3 1.7 copy-start.3
  168.5 67.7 %all-reduce.10.cloned.1.call-start = ((), (), s32[]{:S(2)}) async-start(), calls=%async_computation.5 | async-start | bytes 1310720 | tf_op jit(solution)/shard_map/psum | solution.py:117
  191.9 18.1 %collective-permute-start.1 = (bf16[64,5120]{1,0:T(8,128)(2,1)S(1)}, bf16[64,5120]{1,0:T(8,128)(2,1)S(1)}, u32[]{:S(2)}, u32[]{:S(2)}) collective-permute-start(bf16[64,5120]{1,0:T(8,128)(2,1)S(1)} %get-tuple-element.21), channel_id=1, source_target_pairs={{0,2},{1,3},{4,6},{5,7},{8,10},{9,11},{12,14},{13,15},{16,18},{17,... | collective-permute-start | bytes 1966088 | tf_op jit(solution)/shard_map/ppermute | solution.py:18
  195.6 14.5 %copy-start.15 = (bf16[16,8,5120]{2,1,0:T(8,128)(2,1)S(1)}, bf16[16,8,5120]{2,1,0:T(8,128)(2,1)}, u32[]{:S(2)}) copy-start(bf16[16,8,5120]{2,1,0:T(8,128)(2,1)} %copy-done.12) | copy-start | bytes 3932164
  195.6 14.5 %copy-start.25 = (bf16[1,64,5120]{2,1,0:T(8,128)(2,1)S(1)}, bf16[1,64,5120]{2,1,0:T(8,128)(2,1)}, u32[]{:S(2)}) copy-start(bf16[1,64,5120]{2,1,0:T(8,128)(2,1)} %constant_dynamic-slice_fusion.8) | copy-start | bytes 1966084
  210.1 2.0 copy-start.9
  212.0 1.9 copy-start.4
  215.4 50.0 %all-reduce.12.cloned.1.call-start = ((), (), s32[]{:S(2)}) async-start(), calls=%async_computation.6 | async-start | bytes 1310720 | tf_op jit(solution)/shard_map/psum | solution.py:144
  218.4 17.8 %copy-start.22 = (bf16[64,5120]{1,0:T(8,128)(2,1)S(1)}, bf16[64,5120]{1,0:T(8,128)(2,1)}, u32[]{:S(2)}) copy-start(bf16[64,5120]{1,0:T(8,128)(2,1)} %copy-done.21) | copy-start | bytes 1966084
  239.3 2.4 copy-start.5
  241.8 1.7 copy-start.10
  245.3 67.4 %all-reduce.14.cloned.1.call-start = ((), (), s32[]{:S(2)}) async-start(), calls=%async_computation.7 | async-start | bytes 1310720 | tf_op jit(solution)/shard_map/psum | solution.py:144
  265.4 2.1 copy-start.24
  269.2 18.8 %collective-permute-start.2 = (bf16[64,5120]{1,0:T(8,128)(2,1)S(1)}, bf16[64,5120]{1,0:T(8,128)(2,1)S(1)}, u32[]{:S(2)}, u32[]{:S(2)}) collective-permute-start(bf16[64,5120]{1,0:T(8,128)(2,1)S(1)} %fusion.46), channel_id=1, source_target_pairs={{2,0},{3,1},{6,4},{7,5},{10,8},{11,9},{14,12},{15,13},{18,16},{19,... | collective-permute-start | bytes 1966088 | tf_op jit(solution)/shard_map/ppermute | solution.py:18
  288.0 2.0 copy-start.6
  290.0 1.7 copy-start.11
  293.5 144.1 %reduce-scatter.2.cloned.1.call-start = ((), (), s32[]{:S(2)}) async-start(), calls=%async_computation.8 | async-start | bytes 6553600 | tf_op jit(solution)/shard_map/reduce_scatter | solution.py:156
  314.4 20.5 %copy-start.7 = (bf16[1,256,5120]{2,1,0:T(8,128)(2,1)S(1)}, bf16[1,256,5120]{2,1,0:T(8,128)(2,1)}, u32[]{:S(2)}) copy-start(bf16[1,256,5120]{2,1,0:T(8,128)(2,1)} %all-gather.5.cloned.1.call-done) | copy-start | bytes 7864324
  316.1 18.8 %collective-permute-start.3 = (bf16[64,5120]{1,0:T(8,128)(2,1)S(1)}, bf16[64,5120]{1,0:T(8,128)(2,1)S(1)}, u32[]{:S(2)}, u32[]{:S(2)}) collective-permute-start(bf16[64,5120]{1,0:T(8,128)(2,1)S(1)} %fusion.52), channel_id=1, source_target_pairs={{2,0},{3,1},{6,4},{7,5},{10,8},{11,9},{14,12},{15,13},{18,16},{19,... | collective-permute-start | bytes 1966088 | tf_op jit(solution)/shard_map/ppermute | solution.py:18
  (11 other events, 15.3 us)
Sparse Core Ops, SparseCore 0:
  9.6 57.4 all-gather.2
  68.6 53.4 all-gather.4
  125.5 17.5 all-reduce.5
  168.6 20.6 all-reduce.7
  215.5 20.6 all-reduce.9
  245.4 19.9 all-reduce.11
  293.6 19.0 all-reduce.13
  343.3 94.1 reduce-scatter.1
where the time goes:
time: 450 us; the launch traced here: 449 us
  waiting for transfers between devices  326 us (72%)
  local copies, waits for them, and re-layouts  32.9 us (7%)
  other arithmetic  32.2 us (7%)
  matrix products  19.3 us (4%)
  between operations  15.3 us (3%)
  blocking collectives  12.9 us (3%)
  starting transfers between devices  10.5 us (2%)
    reduce_scatter x1, waiting for transfers between devices, local(): lax.psum_scatter(jnp.concatenate([contract_first(flat_normed, flat_grad_v...  80.2 us
    ppermute x4, waiting for transfers between devices, from_behind(): return lax.ppermute(block, axis, route)  57.8 us
    all_gather x1, waiting for transfers between devices, local(): lax.all_gather(output_proj, 'dp', axis=2, tiled=True)  52.5 us
    all_gather x1, waiting for transfers between devices, local(): lax.all_gather(value_proj, 'dp', axis=1, tiled=True)  48.9 us
    psum x3, waiting for transfers between devices, local(): lax.psum(partial_out.astype(jnp.bfloat16), 'tensor').astype(jnp.float32)  48.4 us
    psum x2, waiting for transfers between devices, local(): lax.psum(partial_norm.astype(jnp.bfloat16), 'tensor').astype(jnp.float32)  37 us
    dynamic_update_slice x10, other arithmetic, put_slot(): lax.dynamic_update_index_in_dim(slot_store, jnp.where(active, new_value,...  14.3 us
    psum x1, blocking collectives, local(): token_total = lax.psum(local_count, 'dp')  12.9 us
  transfers between devices with their start and end apart: 12, of which 12 were waited for; matrix products, arithmetic and copies ran while one was open for 6% of the time, Pallas kernels for 0%

commit v1 on v0

--- a/solution.py
+++ b/solution.py
@@ -1,3 +1,4 @@
+import functools
 import math
 import jax
 import jax.numpy as jnp
@@ -10,6 +11,14 @@
 loss_scale = 4096.0
 clip_high = math.log(1.28)
 clip_low = math.log(0.8)
+
+
+def run_supply_all(packet, row_axis):
+    newest = jnp.sum(jax.lax.all_gather(packet, row_axis), axis=0)
+    return newest
+
+
+_render_gates = functools.partial(run_supply_all, row_axis="tensor")
 
 
 def from_behind(block, axis, distance):
@@ -114,7 +123,7 @@
             jnp.bfloat16
         )
         partial_out = jnp.dot(projected, w_second, preferred_element_type=jnp.float32)
-        mixed_sum = lax.psum(partial_out.astype(jnp.bfloat16), "tensor").astype(jnp.float32)
+        mixed_sum = _render_gates(partial_out.astype(jnp.bfloat16)).astype(jnp.float32)
         leaving = (values + mixed_sum).astype(jnp.bfloat16)
         store_in = put_slot(store_in, entering, clamped, active)
         store_normed = put_slot(store_normed, normed, clamped, active)

time: 450 us -> 429 us (0.953)
  waiting for transfers between devices: 326 us -> 298 us
  other arithmetic: 32.2 us -> 39.4 us
    psum x3 -> x0, waiting for transfers between devices: 48.4 us -> none  [local(): lax.psum(partial_out.astype(jnp.bfloat16), 'tensor').astype(jnp.float32)]
    all_gather x0 -> x3, waiting for transfers between devices: none -> 18.3 us  [run_supply_all(): newest = jnp.sum(jax.lax.all_gather(packet, row_axis), axis=0)]
    reduce_sum x0 -> x3, other arithmetic: none -> 6.78 us  [run_supply_all(): newest = jnp.sum(jax.lax.all_gather(packet, row_axis), axis=0)]
    dynamic_update_slice x10 -> x9, other arithmetic: 14.3 us -> 13.3 us  [put_slot(): lax.dynamic_update_index_in_dim(slot_store, jnp.where(active, new_value,...]
    unnamed x65 -> x69, local copies, waits for them, and re-layouts: 11.3 us -> 10.3 us
  transfers between devices with their start and end apart: 12 -> 12, of which waited for: 12 -> 12; matrix products, arithmetic and copies ran while one was open for 6% -> 7% of each run, Pallas kernels for 0% -> 0%
where the time goes in v1:
time: 429 us; the launch traced here: 428 us
  waiting for transfers between devices  298 us (69%)
  other arithmetic  39.4 us (9%)
  local copies, waits for them, and re-layouts  31.9 us (7%)
  matrix products  19.2 us (4%)
  between operations  15.4 us (4%)
  blocking collectives  12.9 us (3%)
  starting transfers between devices  10.6 us (2%)
    reduce_scatter x1, waiting for transfers between devices, local(): lax.psum_scatter(jnp.concatenate([contract_first(flat_normed, flat_grad_v...  80.1 us
    ppermute x4, waiting for transfers between devices, from_behind(): return lax.ppermute(block, axis, route)  58.1 us
    all_gather x1, waiting for transfers between devices, local(): lax.all_gather(output_proj, 'dp', axis=2, tiled=True)  52.5 us
    all_gather x1, waiting for transfers between devices, local(): lax.all_gather(value_proj, 'dp', axis=1, tiled=True)  50.9 us
    psum x2, waiting for transfers between devices, local(): lax.psum(partial_norm.astype(jnp.bfloat16), 'tensor').astype(jnp.float32)  36.8 us
    all_gather x3, waiting for transfers between devices, run_supply_all(): newest = jnp.sum(jax.lax.all_gather(packet, row_axis), axis=0)  18.3 us
    dynamic_update_slice x9, other arithmetic, put_slot(): lax.dynamic_update_index_in_dim(slot_store, jnp.where(active, new_value,...  13.3 us
    psum x1, blocking collectives, local(): token_total = lax.psum(local_count, 'dp')  12.9 us
  transfers between devices with their start and end apart: 12, of which 12 were waited for; matrix products, arithmetic and copies ran while one was open for 7% of the time, Pallas kernels for 0%

profile of v1, /device:TPU:0, one launch (start us, length us, event | category | flops | bytes accessed | tf_op | source)
XLA Modules:
  0.0 427.6 jit_solution(14197899247860070260)
XLA Ops:
  12.9 2.0 broadcast_select_fusion.1
  16.2 50.9 %all-gather.9.cloned.1.call-done = bf16[1,5120,256]{2,1,0:T(8,128)(2,1)} async-done(((bf16[1,1280,256]{2,1,0:T(8,128)(2,1)}), bf16[1,5120,256]{2,1,0:T(8,128)(2,1)}) %all-gather.9.cloned.1.call-update) | async-done | bytes 2621456 | tf_op jit(solution)/shard_map/all_gather | solution.py:91
  67.1 2.6 bitcast_dynamic-update-slice_fusion.9
  69.7 52.5 %all-gather.11.cloned.1.call-done = bf16[1,256,5120]{2,1,0:T(8,128)(2,1)} async-done(((bf16[1,256,1280]{2,1,0:T(8,128)(2,1)}), bf16[1,256,5120]{2,1,0:T(8,128)(2,1)}) %all-gather.11.cloned.1.call-update) | async-done | bytes 2621456 | tf_op jit(solution)/shard_map/all_gather | solution.py:92
  122.2 3.2 convolution_convert_fusion.4
  130.2 3.5 all-gather.13.cloned.1.call-done
  136.9 3.8 collective-permute-start
  141.9 13.2 %collective-permute-done = bf16[64,5120]{1,0:T(8,128)(2,1)S(1)} collective-permute-done((bf16[64,5120]{1,0:T(8,128)(2,1)S(1)}, bf16[64,5120]{1,0:T(8,128)(2,1)S(1)}, u32[]{:S(2)}, u32[]{:S(2)}) %collective-permute-start) | collective-permute-done | bytes 655392 | tf_op jit(solution)/shard_map/ppermute | solution.py:27
  160.7 2.0 constant_dynamic-slice_fusion.14
  162.8 2.0 constant_dynamic-slice_fusion.8
  164.8 7.1 %all-gather.15.cloned.1.call-done = bf16[128,5120]{1,0:T(8,128)(2,1)} async-done(((bf16[64,5120]{1,0:T(8,128)(2,1)}), bf16[128,5120]{1,0:T(8,128)(2,1)}) %all-gather.15.cloned.1.call-update) | async-done | bytes 1310736 | tf_op jit(solution)/shard_map/all_gather | solution.py:17
  171.9 2.6 reduce_sum.138
  174.5 2.5 bitcast_dynamic-update-slice_fusion.4
  177.0 3.7 collective-permute-start.1
  180.7 2.1 constant_dynamic-slice_fusion.13
  182.8 12.2 %collective-permute-done.1 = bf16[64,5120]{1,0:T(8,128)(2,1)S(1)} collective-permute-done((bf16[64,5120]{1,0:T(8,128)(2,1)S(1)}, bf16[64,5120]{1,0:T(8,128)(2,1)S(1)}, u32[]{:S(2)}, u32[]{:S(2)}) %collective-permute-start.1) | collective-permute-done | bytes 655392 | tf_op jit(solution)/shard_map/ppermute | solution.py:27
  204.4 7.6 %all-gather.17.cloned.1.call-done = bf16[128,5120]{1,0:T(8,128)(2,1)} async-done(((bf16[64,5120]{1,0:T(8,128)(2,1)}), bf16[128,5120]{1,0:T(8,128)(2,1)}) %all-gather.17.cloned.1.call-update) | async-done | bytes 1310736 | tf_op jit(solution)/shard_map/all_gather | solution.py:17
  212.0 2.6 reduce_sum.140
  214.6 3.1 bitcast_dynamic-update-slice_fusion.5
  217.7 2.4 fusion.28
  221.8 1.8 convolution_convert_fusion.1
  226.1 17.6 %all-reduce.3.cloned.1.call-done = bf16[64,5120]{1,0:T(8,128)(2,1)} async-done(((bf16[64,5120]{1,0:T(8,128)(2,1)}), bf16[64,5120]{1,0:T(8,128)(2,1)}) %all-reduce.3.cloned.1.call-update) | async-done | bytes 655376 | tf_op jit(solution)/shard_map/psum | solution.py:153
  243.8 2.1 fusion.49
  250.0 16.3 %collective-permute-done.2 = bf16[64,5120]{1,0:T(8,128)(2,1)S(1)} collective-permute-done((bf16[64,5120]{1,0:T(8,128)(2,1)S(1)}, bf16[64,5120]{1,0:T(8,128)(2,1)S(1)}, u32[]{:S(2)}, u32[]{:S(2)}) %collective-permute-start.2) | collective-permute-done | bytes 655392 | tf_op jit(solution)/shard_map/ppermute | solution.py:27
  270.0 1.7 convolution_convert_fusion
  271.9 19.2 %all-reduce.5.cloned.1.call-done = bf16[64,5120]{1,0:T(8,128)(2,1)} async-done(((bf16[64,5120]{1,0:T(8,128)(2,1)}), bf16[64,5120]{1,0:T(8,128)(2,1)}) %all-reduce.5.cloned.1.call-update) | async-done | bytes 655376 | tf_op jit(solution)/shard_map/psum | solution.py:153
  296.9 16.3 %collective-permute-done.3 = bf16[64,5120]{1,0:T(8,128)(2,1)S(1)} collective-permute-done((bf16[64,5120]{1,0:T(8,128)(2,1)S(1)}, bf16[64,5120]{1,0:T(8,128)(2,1)S(1)}, u32[]{:S(2)}, u32[]{:S(2)}) %collective-permute-start.3) | collective-permute-done | bytes 655392 | tf_op jit(solution)/shard_map/ppermute | solution.py:27
  316.6 2.2 fusion.1
  318.8 2.7 pad_maximum_fusion
  322.8 12.9 %psum.23 = f32[]{:T(128)} all-reduce(f32[]{:T(128)} %convert_reduce_fusion), channel_id=1, replica_groups=mesh['groups'=2,'dp'=4,'section'=2,'tensor'=2] {'dp'}, use_global_device_ids=true, to_apply=%region_17.20 | all-reduce | flops 1 | bytes 8 | tf_op jit(solution)/shard_map/psum | solution.py:177
  335.7 80.1 %reduce-scatter.2.cloned.1.call-done = bf16[1280,512]{0,1:T(8,128)(2,1)} async-done(((bf16[5120,512]{0,1:T(8,128)(2,1)}), bf16[1280,512]{0,1:T(8,128)(2,1)}) %reduce-scatter.2.cloned.1.call-update) | async-done | bytes 1310736 | tf_op jit(solution)/shard_map/reduce_scatter | solution.py:165
  415.9 2.2 convert_divide_fusion
  (149 shorter events, 55.5 us)
Async XLA Ops:
  7.2 2.3 copy-start
  7.2 59.9 %all-gather.9.cloned.1.call-start = ((), (), s32[]{:S(2)}) async-start(), calls=%async_computation.1 | async-start | bytes 3276800 | tf_op jit(solution)/shard_map/all_gather | solution.py:91
  7.9 114.3 %all-gather.11.cloned.1.call-start = ((), (), s32[]{:S(2)}) async-start(), calls=%async_computation.2 | async-start | bytes 3276800 | tf_op jit(solution)/shard_map/all_gather | solution.py:92
  8.7 125.0 %all-gather.13.cloned.1.call-start = ((), (), s32[]{:S(2)}) async-start(), calls=%async_computation.6 | async-start | bytes 1966080 | tf_op jit(solution)/shard_map/all_gather | solution.py:17
  12.8 54.2 %copy-start.28 = (f32[1,5120]{1,0:T(1,128)S(1)}, f32[1,5120]{1,0:T(1,128)}, u32[]{:S(2)}) copy-start(f32[1,5120]{1,0:T(1,128)} %param.19) | copy-start | bytes 61444
  122.2 3.3 copy-start.2
  122.2 3.9 copy-start.30
  125.4 46.5 %all-gather.15.cloned.1.call-start = ((), (), s32[]{:S(2)}) async-start(), calls=%async_computation.7 | async-start | bytes 1966080 | tf_op jit(solution)/shard_map/all_gather | solution.py:17
  127.4 1.8 copy-start.13
  135.3 6.5 %copy-start.23 = (bf16[64,5120]{1,0:T(8,128)(2,1)}, bf16[64,5120]{1,0:T(8,128)(2,1)S(1)}, u32[]{:S(2)}) copy-start(bf16[64,5120]{1,0:T(8,128)(2,1)S(1)} %reduce_sum.136) | copy-start | bytes 1966084
  136.9 18.4 %copy-start.14 = (bf16[16,8,5120]{2,1,0:T(8,128)(2,1)S(1)}, bf16[16,8,5120]{2,1,0:T(8,128)(2,1)}, u32[]{:S(2)}) copy-start(bf16[16,8,5120]{2,1,0:T(8,128)(2,1)} %copy-done.12) | copy-start | bytes 3932164
  136.9 18.2 %collective-permute-start = (bf16[64,5120]{1,0:T(8,128)(2,1)S(1)}, bf16[64,5120]{1,0:T(8,128)(2,1)S(1)}, u32[]{:S(2)}, u32[]{:S(2)}) collective-permute-start(bf16[64,5120]{1,0:T(8,128)(2,1)S(1)} %fusion.31), channel_id=1, source_target_pairs={{0,2},{1,3},{4,6},{5,7},{8,10},{9,11},{12,14},{13,15},{16,18},{17,... | collective-permute-start | bytes 1966088 | tf_op jit(solution)/shard_map/ppermute | solution.py:27
  141.9 13.4 %copy-start.24 = (bf16[64,5120]{1,0:T(8,128)(2,1)S(1)}, bf16[64,5120]{1,0:T(8,128)(2,1)}, u32[]{:S(2)}) copy-start(bf16[64,5120]{1,0:T(8,128)(2,1)} %copy-done.23) | copy-start | bytes 1966084
  155.3 2.0 copy-start.8
  157.3 1.7 copy-start.3
  160.4 51.6 %all-gather.17.cloned.1.call-start = ((), (), s32[]{:S(2)}) async-start(), calls=%async_computation.8 | async-start | bytes 1966080 | tf_op jit(solution)/shard_map/all_gather | solution.py:17
  177.0 18.1 %collective-permute-start.1 = (bf16[64,5120]{1,0:T(8,128)(2,1)S(1)}, bf16[64,5120]{1,0:T(8,128)(2,1)S(1)}, u32[]{:S(2)}, u32[]{:S(2)}) collective-permute-start(bf16[64,5120]{1,0:T(8,128)(2,1)S(1)} %get-tuple-element.21), channel_id=1, source_target_pairs={{0,2},{1,3},{4,6},{5,7},{8,10},{9,11},{12,14},{13,15},{16,18},{17,... | collective-permute-start | bytes 1966088 | tf_op jit(solution)/shard_map/ppermute | solution.py:27
  180.7 14.5 %copy-start.15 = (bf16[16,8,5120]{2,1,0:T(8,128)(2,1)S(1)}, bf16[16,8,5120]{2,1,0:T(8,128)(2,1)}, u32[]{:S(2)}) copy-start(bf16[16,8,5120]{2,1,0:T(8,128)(2,1)} %copy-done.12) | copy-start | bytes 3932164
  180.7 14.5 %copy-start.27 = (bf16[1,64,5120]{2,1,0:T(8,128)(2,1)S(1)}, bf16[1,64,5120]{2,1,0:T(8,128)(2,1)}, u32[]{:S(2)}) copy-start(bf16[1,64,5120]{2,1,0:T(8,128)(2,1)} %constant_dynamic-slice_fusion.8) | copy-start | bytes 1966084
  195.2 2.0 copy-start.9
  197.2 1.9 copy-start.4
  200.5 43.3 %all-reduce.3.cloned.1.call-start = ((), (), s32[]{:S(2)}) async-start(), calls=%async_computation.3 | async-start | bytes 1310720 | tf_op jit(solution)/shard_map/psum | solution.py:153
  204.4 10.2 %copy-start.22 = (bf16[64,5120]{1,0:T(8,128)(2,1)S(1)}, bf16[64,5120]{1,0:T(8,128)(2,1)}, u32[]{:S(2)}) copy-start(bf16[64,5120]{1,0:T(8,128)(2,1)} %copy-done.21) | copy-start | bytes 1966084
  217.7 2.4 copy-start.5
  220.1 1.7 copy-start.10
  223.6 67.4 %all-reduce.5.cloned.1.call-start = ((), (), s32[]{:S(2)}) async-start(), calls=%async_computation.4 | async-start | bytes 1310720 | tf_op jit(solution)/shard_map/psum | solution.py:153
  243.7 2.1 copy-start.26
  247.5 18.8 %collective-permute-start.2 = (bf16[64,5120]{1,0:T(8,128)(2,1)S(1)}, bf16[64,5120]{1,0:T(8,128)(2,1)S(1)}, u32[]{:S(2)}, u32[]{:S(2)}) collective-permute-start(bf16[64,5120]{1,0:T(8,128)(2,1)S(1)} %fusion.47), channel_id=1, source_target_pairs={{2,0},{3,1},{6,4},{7,5},{10,8},{11,9},{14,12},{15,13},{18,16},{19,... | collective-permute-start | bytes 1966088 | tf_op jit(solution)/shard_map/ppermute | solution.py:27
  266.3 2.0 copy-start.6
  271.8 144.1 %reduce-scatter.2.cloned.1.call-start = ((), (), s32[]{:S(2)}) async-start(), calls=%async_computation.5 | async-start | bytes 6553600 | tf_op jit(solution)/shard_map/reduce_scatter | solution.py:165
  292.7 20.5 %copy-start.7 = (bf16[1,256,5120]{2,1,0:T(8,128)(2,1)S(1)}, bf16[1,256,5120]{2,1,0:T(8,128)(2,1)}, u32[]{:S(2)}) copy-start(bf16[1,256,5120]{2,1,0:T(8,128)(2,1)} %all-gather.11.cloned.1.call-done) | copy-start | bytes 7864324
  294.5 18.8 %collective-permute-start.3 = (bf16[64,5120]{1,0:T(8,128)(2,1)S(1)}, bf16[64,5120]{1,0:T(8,128)(2,1)S(1)}, u32[]{:S(2)}, u32[]{:S(2)}) collective-permute-start(bf16[64,5120]{1,0:T(8,128)(2,1)S(1)} %fusion.53), channel_id=1, source_target_pairs={{2,0},{3,1},{6,4},{7,5},{10,8},{11,9},{14,12},{15,13},{18,16},{19,... | collective-permute-start | bytes 1966088 | tf_op jit(solution)/shard_map/ppermute | solution.py:27
  (13 other events, 18.3 us)
Sparse Core Ops, SparseCore 0:
  9.6 57.4 all-gather.8
  68.6 53.5 all-gather.10
  125.5 8.1 all-gather.12
  160.6 11.3 all-gather.14
  200.6 11.3 all-gather.16
  223.8 19.9 all-reduce.2
  271.9 19.0 all-reduce.4
  321.7 94.1 reduce-scatter.1
